TPU v7x, 256 devices: a whole 4x4x8 slice. The times are simulated.
256 devices in a mesh: fsdp: 4 (over x), tensor: 4 (over y_lo, core), dp: 16 (over y_hi, z).
Axes of the slice: x: 4, y: 4 (y_hi: 2, y_lo: 2; y = y_hi * 2 + y_lo), z: 8, core: 2. Of those that a mesh axis runs over, the one named last changes fastest.
Arguments:
- tokens: bfloat16 [1024, 8192], P('fsdp', 'dp'), may hold values from -6 to 6
- cotangent: bfloat16 [1024, 8192], P('fsdp', 'dp'), may hold values from -6 to 6
- gate_weight: bfloat16 [8192, 28672], P('fsdp', ('tensor', 'dp')), may hold values from -0.0625 to 0.0625
- up_weight: bfloat16 [8192, 28672], P('fsdp', ('tensor', 'dp')), may hold values from -0.0625 to 0.0625
- down_weight: bfloat16 [28672, 8192], P(('tensor', 'dp'), 'fsdp'), may hold values from -0.03125 to 0.03125
- model_projection: bfloat16 [64, 8192], replicated, may hold values from -0.0625 to 0.0625
- hidden_projection: bfloat16 [64, 28672], P(None, ('tensor', 'dp')), may hold values from -0.03125 to 0.03125
- queries: bfloat16 [256, 12288], P('dp'), may hold values from -0.0546875 to 0.0546875
Outputs:
- scores: float32 [256, 8], P('dp', 'fsdp')
All inputs are finite; a program needn't handle non-finite values.
Results may differ from a plain program's by a relative error of at most 0.003.
Values may be sent and summed in bfloat16 or wider, within the bound.
A program may use at most 128 MiB of HBM per device.

v0:
```python
import jax
import jax.numpy as jnp
from jax import lax
from jax.sharding import PartitionSpec as P

SEQ_LEN = 128


def in_one_piece(arrays, axis, dim, along):
    both = jnp.concatenate(arrays, axis=along)
    out, at, outs = (lax.all_gather(both, axis, axis=dim, tiled=True), 0, [])
    for a in arrays:
        outs.append(lax.slice_in_dim(out, at, at + a.shape[along], axis=along))
        at += a.shape[along]
    return tuple(outs)


def joined_along(pieces, dim):
    lengths = list(pieces.shape[1:])
    lengths[dim] *= pieces.shape[0]
    return jnp.moveaxis(pieces, 0, dim).reshape(lengths)


def copy_for_each(x, axis):
    devices = lax.axis_size(axis)
    return lax.all_to_all(jnp.broadcast_to(x[None], (devices, *x.shape)), axis, 0, 0, tiled=True)


def collect(x, axis, dim):
    return joined_along(copy_for_each(x, axis), dim)


def in_one_piece_2(arrays, axis, dim, along):
    both = jnp.concatenate(arrays, axis=along)
    out, at, outs = (collect(both, axis, dim), 0, [])
    for a in arrays:
        outs.append(lax.slice_in_dim(out, at, at + a.shape[along], axis=along))
        at += a.shape[along]
    return tuple(outs)


def filled_up(lines, devices):
    spare = -len(lines) % devices
    return jnp.pad(lines, [(0, spare)] + [(0, 0)] * (lines.ndim - 1))


def in_blocks(x, dim, devices):
    before, after = (x.shape[:dim], x.shape[dim + 1 :])
    return jnp.moveaxis(x.reshape(*before, devices, -1, *after), dim, 0)


def sum_at_owner(x, axis, dim):
    pieces = in_blocks(x, dim, lax.axis_size(axis))
    arrived = lax.all_to_all(pieces, axis, split_axis=0, concat_axis=0, tiled=True)
    return arrived.sum(axis=0)


def nested_sum(x, axes):
    lines = x.reshape(-1)
    padded = filled_up(lines, lax.axis_size(axes))
    whole = collect(sum_at_owner(padded, axes, 0), axes, 0)
    return lax.slice_in_dim(whole, 0, len(lines)).reshape(x.shape)


def right_dot(left, right):
    return lax.dot_general(
        left, right, (((1,), (1,)), ((), ())), preferred_element_type=jnp.float32
    )


def on_device(
    tokens,
    cotangent,
    gate_weight,
    up_weight,
    down_weight,
    model_projection,
    hidden_projection,
    queries,
):
    full_tok, full_cot = in_one_piece((tokens, cotangent), "dp", 1, 0)
    row_count = full_tok.shape[0]
    pieces = in_one_piece_2((gate_weight, up_weight), "fsdp", 0, 1)
    columns = full_tok
    gate_pre = jnp.dot(columns, pieces[0], preferred_element_type=jnp.float32)
    up_pre = jnp.dot(columns, pieces[1], preferred_element_type=jnp.float32)
    columns = full_cot
    back_grad = right_dot(columns, collect(down_weight, "fsdp", 1))
    sigmoid_gate = jax.nn.sigmoid(gate_pre)
    activated = gate_pre * sigmoid_gate
    hidden = (activated * up_pre).astype(jnp.bfloat16)
    grad_gate = (
        back_grad * up_pre * sigmoid_gate * (1.0 + gate_pre * (1.0 - sigmoid_gate))
    ).astype(jnp.bfloat16)
    grad_up = (back_grad * activated).astype(jnp.bfloat16)
    model_tok = right_dot(full_tok, model_projection)
    model_cot = right_dot(full_cot, model_projection)
    stacked = jnp.concatenate((grad_gate, grad_up, hidden), axis=0)
    projected = right_dot(stacked, hidden_projection)
    rank_size = model_projection.shape[0]
    seq_count = row_count // SEQ_LEN

    def shaped(matrix):
        return matrix.reshape(seq_count, SEQ_LEN, rank_size)

    proj_gate = shaped(projected[:row_count])
    proj_up = shaped(projected[row_count : 2 * row_count])
    proj_hidden = shaped(projected[2 * row_count :])
    high = lax.Precision.HIGHEST
    g_gate = jnp.einsum("sti,stj->sij", shaped(model_tok), proj_gate, precision=high)
    g_up = jnp.einsum("sti,stj->sij", shaped(model_tok), proj_up, precision=high)
    g_down = jnp.einsum("sti,stj->sij", proj_hidden, shaped(model_cot), precision=high)
    grads = jnp.stack((g_gate, g_up, g_down), axis=1).reshape(seq_count, 3 * rank_size * rank_size)
    summed_grads = nested_sum(grads, ("tensor", "dp"))
    scores = jnp.dot(queries.astype(jnp.float32), summed_grads.T, precision=high)
    return scores


def solution(mesh):
    return jax.shard_map(
        on_device,
        mesh=mesh,
        in_specs=(
            P("fsdp", "dp"),
            P("fsdp", "dp"),
            P("fsdp", ("tensor", "dp")),
            P("fsdp", ("tensor", "dp")),
            P(("tensor", "dp"), "fsdp"),
            P(),
            P(None, ("tensor", "dp")),
            P("dp", None),
        ),
        out_specs=P("dp", "fsdp"),
        check_vma=False,
    )
```

profile of v0, /device:TPU:1, one launch (start us, length us, event | category | flops | bytes accessed | tf_op | source)
XLA Modules:
  0.0 345.2 jit_solution(12982610159245683790)
XLA Ops:
  6.5 0.0 copy-start
  6.5 5.5 %broadcast_in_dim.6 = bf16[4,448,2048]{2,1,0:T(8,128)(2,1)} broadcast(bf16[448,2048]{1,0:T(8,128)(2,1)} %param.12), dimensions={1,2} | broadcast | bytes 9175040 | tf_op jit(solution)/shard_map/broadcast_in_dim | solution.py:26
  12.0 5.5 %all-to-all-start = ((bf16[4,448,2048]{2,1,0:T(8,128)(2,1)}), bf16[4,448,2048]{2,1,0:T(8,128)(2,1)}, u32[]{:S(2)}, u32[]{:S(2)}) async-start(bf16[4,448,2048]{2,1,0:T(8,128)(2,1)} %broadcast_in_dim.6), calls=%async_computation | async-start | bytes 14680064 | tf_op jit(solution)/shard_map/all_to_all | solution.py:26
  17.6 0.0 all-gather.2.cloned.1.call-start
  17.7 0.9 pad_maximum_fusion.1
  18.5 0.0 all-gather.2.cloned.1.call-update
  18.5 3.8 %pad_maximum_fusion = bf16[2048,896]{0,1:T(8,128)(2,1)} fusion(bf16[2048,448]{0,1:T(8,128)(2,1)S(1)} %copy-done.2, bf16[2048,448]{0,1:T(8,128)(2,1)} %param.10), kind=kLoop, calls=%fused_computation.8 | loop fusion | flops 7340032 | bytes 7340032 | tf_op jit(solution)/shard_map/concatenate | solution.py:34
  22.4 6.1 %copy.25 = bf16[2048,896]{1,0:T(8,128)(2,1)} copy(bf16[2048,896]{0,1:T(8,128)(2,1)} %pad_maximum_fusion) | data formatting | bytes 7340032 | tf_op jit(solution)/shard_map/concatenate | solution.py:34
  28.5 69.8 %all-to-all-done = bf16[4,448,2048]{2,1,0:T(8,128)(2,1)} async-done(((bf16[4,448,2048]{2,1,0:T(8,128)(2,1)}), bf16[4,448,2048]{2,1,0:T(8,128)(2,1)}, u32[]{:S(2)}, u32[]{:S(2)}) %all-to-all-start) | async-done | bytes 7340064 | tf_op jit(solution)/shard_map/all_to_all | solution.py:26
  98.3 6.7 %broadcast_in_dim.7 = bf16[4,2048,896]{2,1,0:T(8,128)(2,1)} broadcast(bf16[2048,896]{1,0:T(8,128)(2,1)} %copy.25), dimensions={1,2} | broadcast | bytes 18350080 | tf_op jit(solution)/shard_map/broadcast_in_dim | solution.py:26
  105.1 6.8 %all-to-all-start.1 = ((bf16[4,2048,896]{2,1,0:T(8,128)(2,1)}), bf16[4,2048,896]{2,1,0:T(8,128)(2,1)}, u32[]{:S(2)}, u32[]{:S(2)}) async-start(bf16[4,2048,896]{2,1,0:T(8,128)(2,1)} %broadcast_in_dim.7), calls=%async_computation.1 | async-start | bytes 29360128 | tf_op jit(solution)/shard_map/all_to_all | solution.py:26
  111.9 7.4 %copy.39 = bf16[4,56,8,2048]{3,2,0,1:T(8,128)(2,1)} copy(bf16[4,56,8,2048]{3,2,1,0:T(8,128)(2,1)} %bitcast.16) | data formatting | bytes 14680064 | tf_op jit(solution)/shard_map/reshape | solution.py:21
  119.4 150.3 %all-to-all-done.1 = bf16[4,2048,896]{2,1,0:T(8,128)(2,1)} async-done(((bf16[4,2048,896]{2,1,0:T(8,128)(2,1)}), bf16[4,2048,896]{2,1,0:T(8,128)(2,1)}, u32[]{:S(2)}, u32[]{:S(2)}) %all-to-all-start.1) | async-done | bytes 14680096 | tf_op jit(solution)/shard_map/all_to_all | solution.py:26
  269.6 11.6 %fusion.2 = f32[256,448]{0,1:T(8,128)S(1)} fusion(bf16[8192,896]{1,0:T(8,128)(2,1)} %bitcast.1, bf16[512,8192]{1,0:T(8,128)(2,1)} %all-gather.2.cloned.1.call-done), kind=kOutput, calls=%fused_computation.2 | convolution fusion | flops 1879048192 | bytes 13041664 | tf_op jit(solution)/shard_map/dot_general | solution.py:86
  281.3 2.1 fusion.6
  283.4 0.0 copy-start.7
  283.4 7.1 %multiply_convert_fusion.2 = (bf16[256,448]{0,1:T(8,128)(2,1)S(1)}, bf16[256,448]{0,1:T(8,128)(2,1)S(1)}, bf16[256,448]{0,1:T(8,128)(2,1)S(1)}) fusion(f32[256,448]{0,1:T(8,128)S(1)} %fusion.6, f32[256,448]{0,1:T(8,128)S(1)} %fusion.2, bf16[8192,896]{1,0:T(8,128)(2,1)} %bitcast.1, bf16[512,8192]{1,0:T(8,128)(2,1)S(1)} %copy-done.5), kind=kOutput, calls=%fused_computation.28 | convolution fusion | flops 1880768512 | bytes 14188544 | tf_op jit(solution)/shard_map/dot_general | solution.py:85
  290.5 0.2 fusion.18
  290.7 0.0 copy-start.6
  290.8 1.4 fusion.12
  292.1 0.2 convolution_bitcast_fusion.2
  292.4 0.2 convolution_bitcast_fusion.1
  292.6 1.4 fusion.15
  294.0 0.2 convolution_bitcast_fusion
  294.3 0.2 all_to_all.21
  294.5 28.1 %all_to_all.26 = f32[64,1,384]{2,1,0:T(1,128)S(1)} all-to-all(f32[64,1,384]{2,1,0:T(1,128)S(1)} %all_to_all.21), channel_id=1, replica_groups=mesh['fsdp'=4,'tensor'=4,'dp'=16] {'tensor','dp'}, dimensions={0} | all-to-all | bytes 196608 | tf_op jit(solution)/shard_map/all_to_all | solution.py:54
  322.5 0.1 reduce_sum.9
  322.6 0.1 broadcast_in_dim.8
  322.7 14.3 %all_to_all.27 = f32[64,1,384]{2,1,0:T(1,128)S(1)} all-to-all(f32[64,1,384]{2,1,0:T(1,128)S(1)} %broadcast_in_dim.8), channel_id=1, replica_groups=mesh['fsdp'=4,'tensor'=4,'dp'=16] {'tensor','dp'}, dimensions={0} | all-to-all | bytes 196608 | tf_op jit(solution)/shard_map/all_to_all | solution.py:26
  337.0 0.2 reduce.1
  337.2 0.1 reshape_reshape.4
  337.3 1.1 convolution_bitcast_fusion.3
  (17 shorter events, 0.1 us)
Async XLA Ops:
  6.5 284.2 %copy-start = (bf16[64,8192]{1,0:T(8,128)(2,1)S(1)}, bf16[64,8192]{1,0:T(8,128)(2,1)}, u32[]{:S(2)}) copy-start(bf16[64,8192]{1,0:T(8,128)(2,1)} %param.13) | copy-start | bytes 3145732
  12.0 5.6 %copy-start.3 = (bf16[256,512]{1,0:T(8,128)(2,1)S(1)}, bf16[256,512]{1,0:T(8,128)(2,1)}, u32[]{:S(2)}) copy-start(bf16[256,512]{1,0:T(8,128)(2,1)} %param.9) | copy-start | bytes 786436
  12.0 5.6 %copy-start.4 = (bf16[256,512]{1,0:T(8,128)(2,1)S(1)}, bf16[256,512]{1,0:T(8,128)(2,1)}, u32[]{:S(2)}) copy-start(bf16[256,512]{1,0:T(8,128)(2,1)} %param.8) | copy-start | bytes 786436
  12.0 6.5 %copy-start.2 = (bf16[2048,448]{0,1:T(8,128)(2,1)S(1)}, bf16[2048,448]{0,1:T(8,128)(2,1)}, u32[]{:S(2)}) copy-start(bf16[2048,448]{0,1:T(8,128)(2,1)} %param.11) | copy-start | bytes 5505028
  12.0 86.3 %all-to-all-start = ((bf16[4,448,2048]{2,1,0:T(8,128)(2,1)}), bf16[4,448,2048]{2,1,0:T(8,128)(2,1)}, u32[]{:S(2)}, u32[]{:S(2)}) async-start(bf16[4,448,2048]{2,1,0:T(8,128)(2,1)} %broadcast_in_dim.6), calls=%async_computation | async-start | bytes 14680064 | tf_op jit(solution)/shard_map/all_to_all | solution.py:26
  17.6 252.1 %all-gather.2.cloned.1.call-start = ((), (), s32[]{:S(2)}) async-start(), calls=%async_computation.4 | async-start | bytes 8912896 | tf_op jit(solution)/shard_map/all_gather | solution.py:11
  105.1 164.6 %all-to-all-start.1 = ((bf16[4,2048,896]{2,1,0:T(8,128)(2,1)}), bf16[4,2048,896]{2,1,0:T(8,128)(2,1)}, u32[]{:S(2)}, u32[]{:S(2)}) async-start(bf16[4,2048,896]{2,1,0:T(8,128)(2,1)} %broadcast_in_dim.7), calls=%async_computation.1 | async-start | bytes 29360128 | tf_op jit(solution)/shard_map/all_to_all | solution.py:26
  269.6 11.6 %copy-start.1 = (bf16[4,56,8,2048]{3,2,0,1:T(8,128)(2,1)S(1)}, bf16[4,56,8,2048]{3,2,0,1:T(8,128)(2,1)}, u32[]{:S(2)}) copy-start(bf16[4,56,8,2048]{3,2,0,1:T(8,128)(2,1)} %copy.39) | copy-start | bytes 22020100
  269.6 11.6 %copy-start.5 = (bf16[512,8192]{1,0:T(8,128)(2,1)S(1)}, bf16[512,8192]{1,0:T(8,128)(2,1)}, u32[]{:S(2)}) copy-start(bf16[512,8192]{1,0:T(8,128)(2,1)} %all-gather.2.cloned.1.call-done) | copy-start | bytes 25165828
  283.4 7.1 %copy-start.7 = (bf16[64,448]{1,0:T(8,128)(2,1)S(1)}, bf16[64,448]{1,0:T(8,128)(2,1)}, u32[]{:S(2)}) copy-start(bf16[64,448]{1,0:T(8,128)(2,1)} %param.14) | copy-start | bytes 172036
  290.7 46.5 %copy-start.6 = (bf16[16,12288]{1,0:T(8,128)(2,1)S(1)}, bf16[16,12288]{1,0:T(8,128)(2,1)}, u32[]{:S(2)}) copy-start(bf16[16,12288]{1,0:T(8,128)(2,1)} %param.15) | copy-start | bytes 1179652
Sparse Core Ops, SparseCore 0:
  20.9 147.8 all-gather.1
where the time goes:
time: 346 us; the launch traced here: 345 us
  waiting for transfers between devices  220 us (64%)
  blocking collectives  42.4 us (12%)
  local copies, waits for them, and re-layouts  26.1 us (8%)
  matrix products  25.6 us (7%)
  between operations  13.6 us (4%)
  starting transfers between devices  12.4 us (4%)
  other arithmetic  5.04 us (1%)
    all_to_all x2, waiting for transfers between devices, copy_for_each(): lax.all_to_all(jnp.broadcast_to(x[None], (devices, *x.shape)), axis, 0, 0...  220 us
    all_to_all x1, blocking collectives, sum_at_owner(): lax.all_to_all(pieces, axis, split_axis=0, concat_axis=0, tiled=True)  28.1 us
    all_to_all x1, blocking collectives, copy_for_each(): lax.all_to_all(jnp.broadcast_to(x[None], (devices, *x.shape)), axis, 0, 0...  14.3 us
    all_to_all x2, starting transfers between devices, copy_for_each(): lax.all_to_all(jnp.broadcast_to(x[None], (devices, *x.shape)), axis, 0, 0...  12.4 us
    broadcast_in_dim x3, local copies, waits for them, and re-layouts, copy_for_each(): jnp.broadcast_to(x[None], (devices, *x.shape))  12.3 us
    dot_general x1, matrix products, on_device(): up_pre = jnp.dot(columns, pieces[1], preferred_element_type=jnp.float32)  11.6 us
    reshape x1, local copies, waits for them, and re-layouts, joined_along(): return jnp.moveaxis(pieces, 0, dim).reshape(lengths)  7.44 us
    dot_general x1, matrix products, on_device(): gate_pre = jnp.dot(columns, pieces[0], preferred_element_type=jnp.float32)  7.07 us
  transfers between devices with their start and end apart: 3, of which 2 were waited for; matrix products, arithmetic and copies ran while one was open for 7% of the time, Pallas kernels for 0%

commit v1 on v0

v1 whole, which is shorter than its diff:
```python
import jax
import jax.numpy as jnp
from jax import lax
from jax.experimental import pallas as pl
from jax.experimental.pallas import tpu as pltpu
from jax.sharding import PartitionSpec as P

MESH = pl.DeviceIdType.MESH
F32, BF16 = jnp.float32, jnp.bfloat16
SEQ_LEN = 128
NX, NY, NZ = 4, 4, 8
UP, DOWN = 2.0**40, 2.0**-20


def dot(a, b):
    return lax.dot_general(a, b, (((1,), (0,)), ((), ())), preferred_element_type=F32)


def dot_t(a, b):
    return lax.dot_general(a, b, (((1,), (1,)), ((), ())), preferred_element_type=F32)


def exact_dot(a, b):
    return lax.dot_general(
        a, b, (((1,), (0,)), ((), ())), precision=lax.Precision.HIGHEST, preferred_element_type=F32
    )


def encoded(v):
    return ((v * UP) * jnp.abs(v) * ((v * UP) * v)).astype(BF16)


def decoded(c):
    c = c.astype(F32)
    root = lax.rsqrt(lax.rsqrt(jnp.maximum(jnp.abs(c), 1e-37))) * DOWN
    return jnp.where(c < 0, -root, root)


def layer(gate, up, back):
    sig = jax.nn.sigmoid(gate)
    act = gate * sig
    hidden = (act * up).astype(BF16)
    grad_gate = (back * up * sig * (1.0 + gate * (1.0 - sig))).astype(BF16)
    grad_up = (back * act).astype(BF16)
    return grad_gate, grad_up, hidden


def kernel(
    tok, cot, wg, wu, wd, mp, hp, qs, out,
    loc, full, wg_v, wu_v, w_gu, wd_v, lb, lm, hpz, qv,
    enc, rh, rx, acc, ml, g_tmp, gpart, r8, s24, rz, gs,
    ld_sem, a_sem, b1_sem, b2_sem, c_sem, e_sem, d_sem, snd_sem, xs_sem, rh_sem, rx_sem, ml_sem, r8_sem, rz_sem, gs_sem,
):
    x = lax.axis_index("fsdp")
    t = lax.axis_index("tensor")
    d = lax.axis_index("dp")
    k, ylo = lax.rem(t, 2), t // 2
    yhi, z = d // NZ, lax.rem(d, NZ)
    y = yhi * 2 + ylo
    sib = 1 - k

    def dev(x_, y_, z_, k_):
        return (x_, lax.rem(y_, 2) * 2 + k_, (y_ // 2) * NZ + z_)

    def off(v, o, n):
        return lax.rem(v + o, n)

    def remote(src, dst, ssem, rsem, to):
        return pltpu.make_async_remote_copy(
            src_ref=src, dst_ref=dst, send_sem=ssem, recv_sem=rsem, device_id=to, device_id_type=MESH
        )

    def local(src, dst, sem):
        return pltpu.make_async_copy(src, dst, sem)

    def wait(ref, sem):
        pltpu.make_async_copy(ref, ref, sem).wait()

    @pl.when(k == 0)
    def _():
        local(tok, loc, ld_sem.at[0]).start()

    @pl.when(k == 1)
    def _():
        local(cot, loc, ld_sem.at[0]).start()

    depth = w_gu.shape[0]
    loads = [
        local(wg, wg_v, ld_sem.at[1]),
        local(wu, wu_v, ld_sem.at[2]),
        local(wd.at[pl.ds(0, 384)], wd_v, ld_sem.at[3]),
        local(wd.at[pl.ds(384, 64)], lb.at[pl.ds(0, 64)], ld_sem.at[4]),
        local(mp.at[:, pl.ds(pl.multiple_of(x * depth, depth), depth)], lm.at[pl.ds(64, 64)], ld_sem.at[5]),
        local(hp, hpz.at[pl.ds(64, 64)], ld_sem.at[6]),
        local(qs, qv, ld_sem.at[7]),
    ]
    for c in loads:
        c.start()

    barrier = pltpu.get_barrier_semaphore()
    peers = [
        dev(off(x, ox, NX), off(y, oy, NY), z, k) for ox in range(NX) for oy in range(NY) if ox or oy
    ]
    peers += [dev(x, y, off(z, oz, NZ), k) for oz in range(1, NZ)]
    peers += [dev(x, off(y, oy, NY), z, sib) for oy in range(NY)]
    for p in peers:
        pl.semaphore_signal(barrier, inc=1, device_id=p, device_id_type=MESH)
    pl.semaphore_wait(barrier, len(peers))

    def rows(r, q, part=0, n=64):
        return pl.ds(pl.multiple_of(r * 256 + q * 64 + part, 32), n)

    local(tok, loc, ld_sem.at[0]).wait()
    xt = 2 * yhi + z // 4
    y2 = off(y, 2 * ylo + 3, NY)
    col = pl.ds(pl.multiple_of(lax.rem(z, 4) * 512, 512), 512)

    def quarter(q):
        return loc.at[pl.ds(pl.multiple_of(q * 64, 64), 64)]

    a2 = remote(quarter(y2), full.at[k, rows(x, y2), col], snd_sem.at[0], a_sem.at[x], dev(xt, y2, z, k))
    a2.start()
    a1 = remote(quarter(y), full.at[k, rows(x, y), col], snd_sem.at[1], a_sem.at[x], dev(xt, y, z, k))

    @pl.when(xt != x)
    def _():
        a1.start()

    @pl.when(xt == x)
    def _():
        local(quarter(y), full.at[k, rows(x, y), col], a_sem.at[x]).start()

    for c in loads:
        c.wait()
    w_gu[:, 0:384] = wg_v[:, 0:384]
    w_gu[:, 384:768] = wu_v[:, 0:384]
    ri = lax.broadcasted_iota(jnp.int32, (64, 128), 0)
    ci = lax.broadcasted_iota(jnp.int32, (64, 128), 1)
    first = jnp.where(ri == ci, 1.0, 0.0).astype(BF16)
    second = jnp.where(ri + 64 == ci, 1.0, 0.0).astype(BF16)
    w_gu[:, 768:896] = (dot(wg_v[:, 384:448], first) + dot(wu_v[:, 384:448], second)).astype(BF16)
    lb[64:128, :] = jnp.zeros((64, depth), BF16)
    lm[0:64, :] = jnp.zeros((64, depth), BF16)
    hpz[0:64, :] = jnp.zeros((64, 448), BF16)
    hpz[128:192, :] = jnp.zeros((64, 448), BF16)

    order = (2, 1, 3, 0)
    rs = [off(x, o, NX) for o in order]
    zb = 4 * lax.rem(x, 2)
    is_src = z // 4 == lax.rem(x, 2)
    is_far = z // 4 != lax.rem(x, 2)
    far = lax.rem(z - zb + NZ, NZ)
    j = lax.rem(z, 4)

    @pl.when(is_src)
    def _():
        for r in rs:
            piece = full.at[k, rows(r, y), col]
            wait(piece, a_sem.at[r])
            targets = [zb + lax.rem(j + o, 4) for o in (1, 2, 3)]
            targets += [lax.rem(zb + 6 - 2 * (j // 2) + o, NZ) for o in (0, 1)]
            for zt in targets:
                remote(piece, piece, snd_sem.at[2], b1_sem.at[r], dev(x, y, zt, k)).start()

    def z_stage(i):
        r = rs[i]

        @pl.when(is_src)
        def _():
            wait(full.at[k, rows(r, y), pl.ds(0, 1536)], b1_sem.at[r])

        @pl.when(is_far)
        def _():
            wait(full.at[k, rows(r, y), pl.ds(0, 1024)], b1_sem.at[r])

            @pl.when(far == 5)
            def _():
                ref = full.at[k, rows(r, y), pl.ds(1024, 1024)]
                for o in (6, 7):
                    remote(ref, ref, snd_sem.at[3], b2_sem.at[r], dev(x, y, lax.rem(zb + o, NZ), k)).start()

            @pl.when(far == 6)
            def _():
                ref = full.at[k, rows(r, y), pl.ds(0, 1024)]
                for o in (5, 4):
                    remote(ref, ref, snd_sem.at[3], b2_sem.at[r], dev(x, y, lax.rem(zb + o, NZ), k)).start()

            wait(full.at[k, rows(r, y), pl.ds(0, 1024)], b2_sem.at[r])

    yp, ym, yo = off(y, 1, NY), off(y, 3, NY), off(y, 2, NY)

    def to_sibling(r, q):
        ref = full.at[k, rows(r, q)]
        remote(ref, ref, snd_sem.at[6], d_sem.at[r], dev(x, y, z, sib)).start()

    def y_send(i):
        r = rs[i]
        ref = full.at[k, rows(r, y)]
        remote(ref, ref, snd_sem.at[4], c_sem.at[0, r], dev(x, yp, z, k)).start()
        remote(ref, ref, snd_sem.at[4], c_sem.at[1, r], dev(x, ym, z, k)).start()
        to_sibling(r, y)

    def y_pass(i):
        r = rs[i]
        wait(full.at[k, rows(r, ym)], c_sem.at[0, r])
        ref = full.at[k, rows(r, ym, 0, 32)]
        remote(ref, ref, snd_sem.at[5], e_sem.at[0, r], dev(x, yp, z, k)).start()
        to_sibling(r, ym)
        wait(full.at[k, rows(r, yp)], c_sem.at[1, r])
        ref = full.at[k, rows(r, yp, 32, 32)]
        remote(ref, ref, snd_sem.at[5], e_sem.at[1, r], dev(x, ym, z, k)).start()
        to_sibling(r, yp)

    def y_done(i):
        r = rs[i]
        wait(full.at[k, rows(r, yo, 0, 32)], e_sem.at[0, r])
        wait(full.at[k, rows(r, yo, 32, 32)], e_sem.at[1, r])
        to_sibling(r, yo)
        wait(full.at[sib, pl.ds(pl.multiple_of(r * 256, 256), 256)], d_sem.at[r])

    def multiply(i, slot):
        block = pl.ds(pl.multiple_of(rs[i] * 256, 256), 256)
        acc[slot, :, 0:896] = dot(full[0, block, :], w_gu[...])
        acc[slot, :, 896:1280] = dot_t(full[1, block, :], wd_v[...])
        acc[slot, :, 1280:1408] = dot_t(full[1, block, :], lb[...]) + dot_t(full[k, block, :], lm[...])

    xp, xm = off(x, 1, NX), off(x, 3, NX)
    sends = []

    def x_send(src, dst, rsem, to):
        c = remote(src, dst, xs_sem.at[len(sends)], rsem, dev(to, y, z, k))
        c.start()
        sends.append(c)

    top, low = pl.ds(0, 128), pl.ds(128, 128)

    z_stage(0)
    y_send(0)
    z_stage(1)
    y_send(1)
    y_pass(0)
    y_done(0)
    multiply(0, 0)
    enc[0, 0:128] = encoded(acc[0, 0:128])
    x_send(enc.at[0, top], rh.at[0], rh_sem.at[0], xp)
    enc[0, 128:256] = encoded(acc[0, 128:256])
    x_send(enc.at[0, low], rh.at[1], rh_sem.at[1], xm)
    z_stage(2)
    y_send(2)
    y_pass(1)
    y_done(1)
    multiply(1, 0)
    enc[1, 128:256] = encoded(acc[0, 128:256])
    x_send(enc.at[1, low], rx.at[0, low], rx_sem.at[0, 1], xp)
    z_stage(3)
    y_send(3)
    y_pass(2)
    y_done(2)
    wait(rh.at[0], rh_sem.at[0])
    enc[1, 0:128] = encoded(acc[0, 0:128] + decoded(rh[0]))
    x_send(enc.at[1, top], rx.at[0, top], rx_sem.at[0, 0], xp)
    multiply(2, 1)
    enc[2, 0:128] = encoded(acc[1, 0:128])
    x_send(enc.at[2, top], rx.at[1, top], rx_sem.at[1, 0], xm)
    wait(rh.at[1], rh_sem.at[1])
    enc[2, 128:256] = encoded(acc[1, 128:256] + decoded(rh[1]))
    x_send(enc.at[2, low], rx.at[1, low], rx_sem.at[1, 1], xm)
    y_pass(3)
    y_done(3)
    multiply(3, 0)

    for s in range(2):
        part = pl.ds(s * 128, 128)
        wait(rx.at[0, part], rx_sem.at[0, s])
        wait(rx.at[1, part], rx_sem.at[1, s])
        acc[0, part] = acc[0, part] + decoded(rx[0, part]) + decoded(rx[1, part])
    ml[0] = acc[0, :, 1280:1408]
    model = remote(ml.at[0], ml.at[1], ml_sem.at[0], ml_sem.at[1], dev(x, y, z, sib))
    model.start()

    lane = lax.broadcasted_iota(jnp.int32, (32, 128), 1) < 64
    projected = []
    for s in range(2):
        part = pl.ds(s * 128, 128)
        gg, gu, hid = layer(acc[0, part, 0:384], acc[0, part, 384:768], acc[0, part, 896:1280])
        left = acc[0, part, 768:896]
        ggl, gul, hil = layer(left, pltpu.roll(left, 64, 1), acc[0, part, 1280:1408])
        pgu = dot_t(gg, hpz[64:192, 0:384]) + dot_t(ggl[:, 0:64], hpz[64:192, 384:448])
        pgu += dot_t(gu, hpz[0:128, 0:384]) + dot_t(gul[:, 0:64], hpz[0:128, 384:448])
        ph = dot_t(hid, hpz[64:192, 0:384]) + dot_t(hil[:, 0:64], hpz[64:192, 384:448])
        projected.append((pgu, ph))
    model.wait()
    for s in range(2):
        part = pl.ds(s * 128, 128)
        pgu, ph = projected[s]
        mine, other = ml[0, part], ml[1, part]
        m_tok = jnp.where(k == 0, mine, other)
        m_cot = jnp.where(k == 0, other, mine)
        g_tmp[0] = exact_dot(m_tok.T, pgu)
        g_tmp[1] = exact_dot(ph.T, m_cot)
        even, odd = g_tmp[0, pl.ds(64, 32, 2), :], g_tmp[0, pl.ds(65, 32, 2), :]
        gpart[s, 0:32] = jnp.where(lane, even, pltpu.roll(odd, 64, 1))
        gpart[s, 32:64] = jnp.where(lane, pltpu.roll(even, 64, 1), odd)
        even, odd = g_tmp[1, pl.ds(0, 32, 2), :], g_tmp[1, pl.ds(1, 32, 2), :]
        gpart[s, 64:96] = jnp.where(lane, pltpu.roll(even, 64, 1), odd)

    def share(q):
        return pl.ds(pl.multiple_of(q * 24, 8), 24)

    near = [(oy, ok) for oy in range(NY) for ok in range(2) if oy or ok]
    for n, (oy, ok) in enumerate(near):
        y_, k_ = off(y, oy, NY), off(k, ok, 2)
        remote(gpart.at[k_, share(y_)], r8.at[n], snd_sem.at[7], r8_sem.at[n], dev(x, y_, z, k_)).start()
    total = gpart[k, share(y)]
    for n in range(7):
        wait(r8.at[n], r8_sem.at[n])
        total += r8[n]
    s24[...] = total
    for n in range(7):
        remote(s24, rz.at[n], snd_sem.at[8], rz_sem.at[n], dev(x, y, off(z, n + 1, NZ), k)).start()
    for n in range(7):
        wait(rz.at[n], rz_sem.at[n])
        total += rz[n]
    gs[k, share(y)] = total
    for n, (oy, ok) in enumerate(near):
        y_, k_ = off(y, oy, NY), off(k, ok, 2)
        ref = gs.at[k, share(y)]
        remote(ref, ref, snd_sem.at[9], gs_sem.at[n], dev(x, y_, z, k_)).start()
    for n in range(7):
        wait(r8.at[n], gs_sem.at[n])

    sums = [jnp.zeros((16, 128), F32), jnp.zeros((16, 128), F32)]
    for p in range(96):
        q = qv[:, p * 128 : (p + 1) * 128].astype(F32)
        for s in range(2):
            sums[s] += q * gs[s, p : p + 1, :]
    two = lax.broadcasted_iota(jnp.int32, (16, 2), 1)
    out[...] = jnp.where(two == 0, sums[0].sum(1, keepdims=True), sums[1].sum(1, keepdims=True))

    a2.wait_send()

    @pl.when(xt != x)
    def _():
        a1.wait_send()

    @pl.when(is_src)
    def _():
        wait(full.at[0, pl.ds(0, 320)], snd_sem.at[2])

    @pl.when((far == 5) | (far == 6))
    def _():
        wait(full.at[0, pl.ds(0, 256)], snd_sem.at[3])

    wait(full.at[0, pl.ds(0, 512)], snd_sem.at[4])
    wait(full.at[0, pl.ds(0, 256)], snd_sem.at[5])
    wait(full.at[0], snd_sem.at[6])
    for c in sends:
        c.wait_send()
    for n in (7, 8, 9):
        wait(r8, snd_sem.at[n])


def on_device(tok, cot, wg, wu, wd, mp, hp, qs):
    depth = wg.shape[0]
    any_ = pl.BlockSpec(memory_space=pl.ANY)
    dma = pltpu.SemaphoreType.DMA
    return pl.pallas_call(
        kernel,
        out_shape=jax.ShapeDtypeStruct((16, 2), F32),
        in_specs=[any_] * 8,
        out_specs=pl.BlockSpec(memory_space=pltpu.VMEM),
        scratch_shapes=[
            pltpu.VMEM((256, 512), BF16),
            pltpu.VMEM((2, 1024, depth), BF16),
            pltpu.VMEM((depth, 448), BF16),
            pltpu.VMEM((depth, 448), BF16),
            pltpu.VMEM((depth, 896), BF16),
            pltpu.VMEM((384, depth), BF16),
            pltpu.VMEM((128, depth), BF16),
            pltpu.VMEM((128, depth), BF16),
            pltpu.VMEM((192, 448), BF16),
            pltpu.VMEM((16, 12288), BF16),
            pltpu.VMEM((3, 256, 1408), BF16),
            pltpu.VMEM((2, 128, 1408), BF16),
            pltpu.VMEM((2, 256, 1408), BF16),
            pltpu.VMEM((2, 256, 1408), F32),
            pltpu.VMEM((2, 256, 128), F32),
            pltpu.VMEM((2, 128, 128), F32),
            pltpu.VMEM((2, 96, 128), F32),
            pltpu.VMEM((7, 24, 128), F32),
            pltpu.VMEM((24, 128), F32),
            pltpu.VMEM((7, 24, 128), F32),
            pltpu.VMEM((2, 96, 128), F32),
            dma((8,)),
            dma((4,)),
            dma((4,)),
            dma((4,)),
            dma((2, 4)),
            dma((2, 4)),
            dma((4,)),
            dma((10,)),
            dma((6,)),
            dma((2,)),
            dma((2, 2)),
            dma((2,)),
            dma((7,)),
            dma((7,)),
            dma((7,)),
        ],
        compiler_params=pltpu.CompilerParams(
            collective_id=0, has_side_effects=True, vmem_limit_bytes=60 * 2**20
        ),
        name="grads_and_scores",
    )(tok, cot, wg, wu, wd, mp, hp, qs)


def solution(mesh):
    return jax.shard_map(
        on_device,
        mesh=mesh,
        in_specs=(
            P("fsdp", "dp"),
            P("fsdp", "dp"),
            P("fsdp", ("tensor", "dp")),
            P("fsdp", ("tensor", "dp")),
            P(("tensor", "dp"), "fsdp"),
            P(),
            P(None, ("tensor", "dp")),
            P("dp", None),
        ),
        out_specs=P("dp", "fsdp"),
        check_vma=False,
    )
```

time: 346 us -> 132 us (0.38)
  waiting for transfers between devices: 220 us -> 0 us
  Pallas kernels: 0 us -> 124 us
  blocking collectives: 42.4 us -> 0 us
  matrix products: 25.6 us -> 0 us
  local copies, waits for them, and re-layouts: 26.1 us -> 7.76 us
  between operations: 13.6 us -> 0.01 us
  starting transfers between devices: 12.4 us -> 0 us
  other arithmetic: 5.04 us -> 0 us
    all_to_all x2 -> x0, waiting for transfers between devices: 220 us -> none  [copy_for_each(): lax.all_to_all(jnp.broadcast_to(x[None], (devices, *x.shape)), axis, 0, 0...]
    pallas_call x0 -> x1, Pallas kernels: none -> 124 us  [on_device(): pl.pallas_call(kernel, out_shape=jax.ShapeDtypeStruct((16, 2), F32), in_s...]
    all_to_all x2 -> x0, blocking collectives: 42.4 us -> none  [the longest x1 28.1 us: sum_at_owner(): lax.all_to_all(pieces, axis, split_axis=0, concat_axis=0, tiled=True)]
    dot_general x10 -> x0, matrix products: 25.6 us -> none  [the longest x1 11.6 us: on_device(): up_pre = jnp.dot(columns, pieces[1], preferred_element_type=jnp.float32)]
    all_to_all x2 -> x0, starting transfers between devices: 12.4 us -> none  [copy_for_each(): lax.all_to_all(jnp.broadcast_to(x[None], (devices, *x.shape)), axis, 0, 0...]
    broadcast_in_dim x3 -> x0, local copies, waits for them, and re-layouts: 12.3 us -> none  [copy_for_each(): jnp.broadcast_to(x[None], (devices, *x.shape))]
    reshape x1 -> x0, local copies, waits for them, and re-layouts: 7.44 us -> none  [joined_along(): return jnp.moveaxis(pieces, 0, dim).reshape(lengths)]
    unnamed x17 -> x4, local copies, waits for them, and re-layouts: 0.05 us -> 6.43 us
  transfers between devices with their start and end apart: 3 -> 0, of which waited for: 2 -> 0; matrix products, arithmetic and copies ran while one was open for 7% -> 0% of each run, Pallas kernels for 0% -> 0%
where the time goes in v1:
time: 132 us
  Pallas kernels  124 us (94%)
  local copies, waits for them, and re-layouts  7.76 us (6%)
    pallas_call x1, Pallas kernels, on_device(): pl.pallas_call(kernel, out_shape=jax.ShapeDtypeStruct((16, 2), F32), in_s...  124 us
    unnamed x4, local copies, waits for them, and re-layouts  6.43 us

profile of v1, /device:TPU:1, one launch (start us, length us, event | category | flops | bytes accessed | tf_op | source)
XLA Modules:
  0.0 132.3 jit_solution(9121513457278050257)
XLA Ops:
  0.0 0.0 copy-start
  0.0 4.0 %copy.9.wg = bf16[2048,448]{1,0:T(8,128)(2,1)} copy(bf16[2048,448]{0,1:T(8,128)(2,1)} %param.10) | data formatting | bytes 3670016 | tf_op args[2]
  4.0 0.0 copy-done
  4.0 2.5 %copy.10.wu = bf16[2048,448]{1,0:T(8,128)(2,1)} copy(bf16[2048,448]{0,1:T(8,128)(2,1)S(1)} %copy-done) | data formatting | bytes 3670016 | tf_op args[3]
  6.4 124.5 %grads_and_scores.1 = f32[16,2]{1,0:T(8,128)} custom-call(bf16[256,512]{1,0:T(8,128)(2,1)} %tok.1, bf16[256,512]{1,0:T(8,128)(2,1)} %cot.1, bf16[2048,448]{1,0:T(8,128)(2,1)} %copy.9.wg, bf16[2048,448]{1,0:T(8,128)(2,1)} %copy.10.wu, bf16[448,2048]{1,0:T(8,128)(2,1)} %wd.1, bf16[64,8192]{1,0:T(8,128)(2,1)} %mp.1, bf16[64,448]{1,0:T(8,128)(2,1)} %hp.1, ...), custom_call_target="tpu_custom_call" | custom-call | tf_op jit(solution)/shard_map/grads_and_scores/pallas_call | solution.py:367
  130.9 1.3 %copy.11 = f32[16,2]{0,1:T(2,128)} copy(f32[16,2]{1,0:T(8,128)} %grads_and_scores.1) | data formatting | bytes 256 | tf_op jit(solution)/shard_map/grads_and_scores/pallas_call | solution.py:367
Async XLA Ops:
  0.0 4.0 %copy-start = (bf16[2048,448]{0,1:T(8,128)(2,1)S(1)}, bf16[2048,448]{0,1:T(8,128)(2,1)}, u32[]{:S(2)}) copy-start(bf16[2048,448]{0,1:T(8,128)(2,1)} %param.11) | copy-start | bytes 5505028

commit v2 on v1

v2 whole, which is shorter than its diff:
```python
import functools

import jax
import jax.numpy as jnp
from jax import lax
from jax.experimental import pallas as pl
from jax.experimental.pallas import tpu as pltpu
from jax.sharding import PartitionSpec as P

MESH = pl.DeviceIdType.MESH
F32, BF16 = jnp.float32, jnp.bfloat16
SEQ_LEN = 128
NX, NY, NZ = 4, 4, 8
UP, DOWN = 2.0**40, 2.0**-20


def dot(a, b):
    return lax.dot_general(a, b, (((1,), (0,)), ((), ())), preferred_element_type=F32)


def dot_t(a, b):
    return lax.dot_general(a, b, (((1,), (1,)), ((), ())), preferred_element_type=F32)


def exact_dot(a, b):
    return lax.dot_general(
        a, b, (((1,), (0,)), ((), ())), precision=lax.Precision.HIGHEST, preferred_element_type=F32
    )


def encoded(v):
    return ((v * UP) * jnp.abs(v) * ((v * UP) * v)).astype(BF16)


def decoded(c):
    c = c.astype(F32)
    root = lax.rsqrt(lax.rsqrt(jnp.maximum(jnp.abs(c), 1e-37))) * DOWN
    return jnp.where(c < 0, -root, root)


def layer(gate, up, back):
    sig = jax.nn.sigmoid(gate)
    act = gate * sig
    hidden = (act * up).astype(BF16)
    grad_gate = (back * up * sig * (1.0 + gate * (1.0 - sig))).astype(BF16)
    grad_up = (back * act).astype(BF16)
    return grad_gate, grad_up, hidden


def kernel(
    tok, cot, wg, wu, wd, mp, hp, qs, out,
    loc, full, w_gu, w_b, hpz, qv,
    enc, rh, rx, acc, ml, g_tmp, gpart, r8, s24, rz, gs,
    ld_sem, a_sem, z_sem, y_sem, d_sem, snd_sem, a_snd, xs_sem, rh_sem, rx_sem, ml_sem, r8_sem, rz_sem, gs_sem,
):
    x = lax.axis_index("fsdp")
    t = lax.axis_index("tensor")
    d = lax.axis_index("dp")
    k, ylo = lax.rem(t, 2), t // 2
    yhi, z = d // NZ, lax.rem(d, NZ)
    y = yhi * 2 + ylo
    sib = 1 - k

    def dev(x_, y_, z_, k_):
        return (x_, lax.rem(y_, 2) * 2 + k_, (y_ // 2) * NZ + z_)

    def off(v, o, n):
        return lax.rem(v + o, n)

    def remote(src, dst, ssem, rsem, to):
        return pltpu.make_async_remote_copy(
            src_ref=src, dst_ref=dst, send_sem=ssem, recv_sem=rsem, device_id=to, device_id_type=MESH
        )

    def local(src, dst, sem):
        return pltpu.make_async_copy(src, dst, sem)

    def wait(ref, sem):
        pltpu.make_async_copy(ref, ref, sem).wait()

    @pl.when(k == 0)
    def _():
        local(tok, loc, ld_sem.at[0]).start()

    @pl.when(k == 1)
    def _():
        local(cot, loc, ld_sem.at[0]).start()

    depth = w_gu.shape[1]
    mp_own = mp.at[:, pl.ds(pl.multiple_of(x * depth, depth), depth)]
    loads = [
        local(wg.at[pl.ds(0, 384)], w_gu.at[pl.ds(0, 384)], ld_sem.at[1]),
        local(wu.at[pl.ds(0, 384)], w_gu.at[pl.ds(384, 384)], ld_sem.at[2]),
        local(wg.at[pl.ds(384, 64)], w_gu.at[pl.ds(768, 64)], ld_sem.at[3]),
        local(wu.at[pl.ds(384, 64)], w_gu.at[pl.ds(832, 64)], ld_sem.at[4]),
        local(mp_own, w_gu.at[pl.ds(960, 64)], ld_sem.at[5]),
        local(wd, w_b.at[pl.ds(0, 448)], ld_sem.at[6]),
        local(mp_own, w_b.at[pl.ds(448, 64)], ld_sem.at[7]),
        local(hp, hpz.at[pl.ds(64, 64)], ld_sem.at[8]),
        local(qs, qv, ld_sem.at[9]),
    ]
    for c in loads:
        c.start()

    barrier = pltpu.get_barrier_semaphore()
    peers = [
        dev(off(x, ox, NX), off(y, oy, NY), z, k) for ox in range(NX) for oy in range(NY) if ox or oy
    ]
    peers += [dev(x, y, off(z, oz, NZ), k) for oz in range(1, NZ)]
    peers += [dev(x, off(y, oy, NY), z, sib) for oy in range(NY)]
    peers += [
        dev(off(x, ox, NX), off(y, oy, NY), off(z, oz, NZ), k)
        for ox in range(NX) for oy in (0, 1, 3) for oz in (1, 2, 6, 7) if ox or oy
    ]
    for p in peers:
        pl.semaphore_signal(barrier, inc=1, device_id=p, device_id_type=MESH)
    pl.semaphore_wait(barrier, len(peers))

    def rows(r, p, part=0, n=128):
        return pl.ds(pl.multiple_of(r * 256 + p * 128 + part, 32), n)

    def piece(r, p, v, part=0, n=64):
        return full.at[k, rows(r, p, lax.rem(v, 2) * 64 + part, n), pl.ds(pl.multiple_of(v // 2 * 512, 512), 512)]

    local(tok, loc, ld_sem.at[0]).wait()
    xt = 2 * yhi + z // 4
    y2 = off(y, 2 * ylo + 3, NY)
    j = lax.rem(z, 4)
    me_p = lax.rem(y, 2)
    a_sends = []
    for n, (yt, u) in enumerate(((y2, 0), (y2, 1), (y, 0), (y, 1))):
        p = lax.rem(yt, 2)
        src = loc.at[pl.ds(pl.multiple_of(p * 128 + u * 64, 64), 64)]
        dst = piece(x, p, 2 * j + u)
        zt = lax.rem(z + j + u + NZ - 2, NZ)
        c = remote(src, dst, a_snd.at[n], a_sem.at[x], dev(xt, yt, zt, k))
        here = (xt == x) & (j + u == 2) if n >= 2 else None
        a_sends.append((c, here))
        if here is None:
            c.start()
        else:

            @pl.when(jnp.logical_not(here))
            def _(c=c):
                c.start()

            @pl.when(here)
            def _(src=src, dst=dst):
                local(src, dst, a_sem.at[x]).start()

    w_gu[896:960, :] = jnp.zeros((64, depth), BF16)
    hpz[0:64, :] = jnp.zeros((64, 448), BF16)
    hpz[128:192, :] = jnp.zeros((64, 448), BF16)

    order = (2, 1, 3, 0)
    rs = [off(x, o, NX) for o in order]
    zb = 4 * lax.rem(x, 2)
    w = lax.rem(z - zb + 2 + NZ, NZ)
    zp, zm = off(z, 1, NZ), off(z, NZ - 1, NZ)
    yp, ym = off(y, 1, NY), off(y, 3, NY)

    def place(o):
        return lax.rem(w + o + NZ, NZ)

    def along_z(ref, up, r, s):
        remote(ref, ref, snd_sem.at[0], z_sem.at[1 - up, r, s], dev(x, y, zp if up else zm, k)).start()

    def along_y(r, v):
        ref = piece(r, me_p, v)
        to = jnp.where(lax.rem(v, 2) == 0, yp, ym)
        remote(ref, ref, snd_sem.at[1], y_sem.at[r], dev(x, to, z, k)).start()

    def z_step(i, s):
        r = rs[i]
        if s == 0:
            own = piece(r, me_p, w)
            wait(own, a_sem.at[r])
            along_z(own, 1, r, 0)
            along_z(own, 0, r, 0)
            along_y(r, w)
        elif s < 4:
            for up in (1, 0):
                v = place(-s if up else s)
                got = piece(r, me_p, v)
                wait(got, z_sem.at[1 - up, r, s - 1])
                if s < 3:
                    along_z(got, up, r, s)
                else:
                    along_z(piece(r, me_p, v, 0 if up else 32, 32), up, r, s)
                along_y(r, v)
        else:
            v = place(4)
            wait(piece(r, me_p, v, 0, 32), z_sem.at[0, r, 3])
            wait(piece(r, me_p, v, 32, 32), z_sem.at[1, r, 3])
            along_y(r, v)
            ref = full.at[k, rows(r, me_p)]
            remote(ref, ref, snd_sem.at[2], d_sem.at[r], dev(x, y, z, sib)).start()

    def y_step(i):
        r = rs[i]
        ref = full.at[k, rows(r, 1 - me_p)]
        wait(ref, y_sem.at[r])
        remote(ref, ref, snd_sem.at[2], d_sem.at[r], dev(x, y, z, sib)).start()

    slots = (0, 1, 2, 0)

    def block(i):
        return pl.ds(pl.multiple_of(rs[i] * 256, 256), 256)

    def multiply_gu(i):
        wait(full.at[sib, block(i)], d_sem.at[rs[i]])
        acc[slots[i], :, 0:1024] = dot_t(full[0, block(i), :], w_gu[...])

    left_lanes = lax.broadcasted_iota(jnp.int32, (256, 128), 1) < 64

    def multiply_b(i):
        slot = slots[i]
        acc[slot, :, 1024:1536] = dot_t(full[1, block(i), :], w_b[...])
        both = acc[slot, :, 1408:1536]
        acc[slot, :, 896:1024] = jnp.where(left_lanes | (k == 1), both, acc[slot, :, 896:1024])

    xp, xm = off(x, 1, NX), off(x, 3, NX)
    sends = []

    def x_send(src, dst, rsem, to):
        c = remote(src, dst, xs_sem.at[len(sends)], rsem, dev(to, y, z, k))
        c.start()
        sends.append(c)

    def x_put(i, h, dst, rsem, to, plus=None):
        part = pl.ds(h * 128, 128)
        v = acc[slots[i], part, 0:1408]
        if plus is not None:
            v = v + decoded(plus)
        enc[i, part] = encoded(v)
        x_send(enc.at[i, part], dst, rsem, to)

    top, low = pl.ds(0, 128), pl.ds(128, 128)

    def x_step(i):
        if i == 0:
            x_put(0, 0, rh.at[0], rh_sem.at[0], xp)
            x_put(0, 1, rh.at[1], rh_sem.at[1], xm)
        elif i == 1:
            x_put(1, 1, rx.at[0, low], rx_sem.at[0, 1], xp)
        elif i == 2:
            x_put(2, 0, rx.at[1, top], rx_sem.at[1, 0], xm)

    def x_last(h):
        wait(rh.at[h], rh_sem.at[h])
        if h == 0:
            x_put(1, 0, rx.at[0, top], rx_sem.at[0, 0], xp, rh[0])
        else:
            x_put(2, 1, rx.at[1, low], rx_sem.at[1, 1], xm, rh[1])

    events = []
    starts = (0, 1, 3, 5)
    for i, at in enumerate(starts):
        for s in range(5):
            events.append((at + s, 0, i, "z%d_%d" % (i, s), functools.partial(z_step, i, s)))
        events.append((at + 5, 1, i, "y%d" % i, functools.partial(y_step, i)))
        events.append((at + 6, 2, i, "gu%d" % i, functools.partial(multiply_gu, i)))
        events.append((at + 7, 2, i, "b%d" % i, functools.partial(multiply_b, i)))
        events.append((at + 7, 3, i, "x%d" % i, functools.partial(x_step, i)))
    events.append((11, 4, 0, "xl0", functools.partial(x_last, 0)))
    events.append((12, 4, 1, "xl1", functools.partial(x_last, 1)))
    events.sort(key=lambda e: e[:3])
    waited = False
    for e in events:
        if e[3] == "gu0":
            for c in loads:
                c.wait()
        with jax.named_scope(e[3]):
            e[4]()

    for s in range(2):
        part = pl.ds(s * 128, 128)
        wait(rx.at[0, part], rx_sem.at[0, s])
        wait(rx.at[1, part], rx_sem.at[1, s])
        acc[0, part, 0:1408] = acc[0, part, 0:1408] + decoded(rx[0, part]) + decoded(rx[1, part])
    ml[0] = acc[0, :, 896:1024]
    model = remote(ml.at[0], ml.at[1], ml_sem.at[0], ml_sem.at[1], dev(x, y, z, sib))
    model.start()

    lane = lax.broadcasted_iota(jnp.int32, (32, 128), 1) < 64
    projected = []
    for s in range(2):
        part = pl.ds(s * 128, 128)
        gg, gu, hid = layer(acc[0, part, 0:384], acc[0, part, 384:768], acc[0, part, 1024:1408])
        left = acc[0, part, 768:896]
        ggl, gul, hil = layer(left, pltpu.roll(left, 64, 1), acc[0, part, 896:1024])
        pgu = dot_t(gg, hpz[64:192, 0:384]) + dot_t(ggl[:, 0:64], hpz[64:192, 384:448])
        pgu += dot_t(gu, hpz[0:128, 0:384]) + dot_t(gul[:, 0:64], hpz[0:128, 384:448])
        ph = dot_t(hid, hpz[64:192, 0:384]) + dot_t(hil[:, 0:64], hpz[64:192, 384:448])
        projected.append((pgu, ph))
    model.wait()
    for s in range(2):
        part = pl.ds(s * 128, 128)
        pgu, ph = projected[s]
        mine, other = ml[0, part], ml[1, part]
        m_tok = jnp.where(k == 0, mine, other)
        m_cot = jnp.where(k == 0, other, mine)
        g_tmp[0] = exact_dot(m_tok.T, pgu)
        g_tmp[1] = exact_dot(ph.T, m_cot)
        even, odd = g_tmp[0, pl.ds(64, 32, 2), :], g_tmp[0, pl.ds(65, 32, 2), :]
        gpart[s, 0:32] = jnp.where(lane, even, pltpu.roll(odd, 64, 1))
        gpart[s, 32:64] = jnp.where(lane, pltpu.roll(even, 64, 1), odd)
        even, odd = g_tmp[1, pl.ds(0, 32, 2), :], g_tmp[1, pl.ds(1, 32, 2), :]
        gpart[s, 64:96] = jnp.where(lane, pltpu.roll(even, 64, 1), odd)

    def share(q):
        return pl.ds(pl.multiple_of(q * 24, 8), 24)

    near = [(oy, ok) for oy in range(NY) for ok in range(2) if oy or ok]
    for n, (oy, ok) in enumerate(near):
        y_, k_ = off(y, oy, NY), off(k, ok, 2)
        remote(gpart.at[k_, share(y_)], r8.at[n], snd_sem.at[7], r8_sem.at[n], dev(x, y_, z, k_)).start()
    total = gpart[k, share(y)]
    for n in range(7):
        wait(r8.at[n], r8_sem.at[n])
        total += r8[n]
    s24[...] = total
    for n in range(7):
        remote(s24, rz.at[n], snd_sem.at[8], rz_sem.at[n], dev(x, y, off(z, n + 1, NZ), k)).start()
    for n in range(7):
        wait(rz.at[n], rz_sem.at[n])
        total += rz[n]
    gs[k, share(y)] = total
    for n, (oy, ok) in enumerate(near):
        y_, k_ = off(y, oy, NY), off(k, ok, 2)
        ref = gs.at[k, share(y)]
        remote(ref, ref, snd_sem.at[9], gs_sem.at[n], dev(x, y_, z, k_)).start()
    for n in range(7):
        wait(r8.at[n], gs_sem.at[n])

    sums = [jnp.zeros((16, 128), F32), jnp.zeros((16, 128), F32)]
    for p in range(96):
        q = qv[:, p * 128 : (p + 1) * 128].astype(F32)
        for s in range(2):
            sums[s] += q * gs[s, p : p + 1, :]
    two = lax.broadcasted_iota(jnp.int32, (16, 2), 1)
    out[...] = jnp.where(two == 0, sums[0].sum(1, keepdims=True), sums[1].sum(1, keepdims=True))

    for c, here in a_sends:
        if here is None:
            c.wait_send()
        else:

            @pl.when(jnp.logical_not(here))
            def _(c=c):
                c.wait_send()

    wait(full.at[0, pl.ds(0, 448)], snd_sem.at[0])
    wait(full.at[0, pl.ds(0, 512)], snd_sem.at[1])
    wait(full.at[0], snd_sem.at[2])
    for c in sends:
        c.wait_send()
    for n in (7, 8, 9):
        wait(r8, snd_sem.at[n])


def on_device(tok, cot, wg, wu, wd, mp, hp, qs):
    depth = wg.shape[0]
    wg, wu = wg.T, wu.T
    any_ = pl.BlockSpec(memory_space=pl.ANY)
    dma = pltpu.SemaphoreType.DMA
    return pl.pallas_call(
        kernel,
        out_shape=jax.ShapeDtypeStruct((16, 2), F32),
        in_specs=[any_] * 8,
        out_specs=pl.BlockSpec(memory_space=pltpu.VMEM),
        scratch_shapes=[
            pltpu.VMEM((256, 512), BF16),
            pltpu.VMEM((2, 1024, depth), BF16),
            pltpu.VMEM((1024, depth), BF16),
            pltpu.VMEM((512, depth), BF16),
            pltpu.VMEM((192, 448), BF16),
            pltpu.VMEM((16, 12288), BF16),
            pltpu.VMEM((3, 256, 1408), BF16),
            pltpu.VMEM((2, 128, 1408), BF16),
            pltpu.VMEM((2, 256, 1408), BF16),
            pltpu.VMEM((3, 256, 1536), F32),
            pltpu.VMEM((2, 256, 128), F32),
            pltpu.VMEM((2, 128, 128), F32),
            pltpu.VMEM((2, 96, 128), F32),
            pltpu.VMEM((7, 24, 128), F32),
            pltpu.VMEM((24, 128), F32),
            pltpu.VMEM((7, 24, 128), F32),
            pltpu.VMEM((2, 96, 128), F32),
            dma((10,)),
            dma((4,)),
            dma((2, 4, 4)),
            dma((4,)),
            dma((4,)),
            dma((10,)),
            dma((4,)),
            dma((6,)),
            dma((2,)),
            dma((2, 2)),
            dma((2,)),
            dma((7,)),
            dma((7,)),
            dma((7,)),
        ],
        compiler_params=pltpu.CompilerParams(
            collective_id=0, has_side_effects=True, vmem_limit_bytes=60 * 2**20
        ),
        name="grads_and_scores",
    )(tok, cot, wg, wu, wd, mp, hp, qs)


def solution(mesh):
    return jax.shard_map(
        on_device,
        mesh=mesh,
        in_specs=(
            P("fsdp", "dp"),
            P("fsdp", "dp"),
            P("fsdp", ("tensor", "dp")),
            P("fsdp", ("tensor", "dp")),
            P(("tensor", "dp"), "fsdp"),
            P(),
            P(None, ("tensor", "dp")),
            P("dp", None),
        ),
        out_specs=P("dp", "fsdp"),
        check_vma=False,
    )
```

time: 132 us -> 94.2 us (0.71)
  Pallas kernels: 124 us -> 92.8 us
  local copies, waits for them, and re-layouts: 7.76 us -> 1.33 us
    pallas_call x1, Pallas kernels: 124 us -> 92.8 us  [on_device(): pl.pallas_call(kernel, out_shape=jax.ShapeDtypeStruct((16, 2), F32), in_s...]
    unnamed x4 -> x0, local copies, waits for them, and re-layouts: 6.43 us -> none
where the time goes in v2:
time: 94.2 us; the launch traced here: 94.1 us
  Pallas kernels  92.8 us (99%)
  local copies, waits for them, and re-layouts  1.33 us (1%)
    pallas_call x1, Pallas kernels, on_device(): pl.pallas_call(kernel, out_shape=jax.ShapeDtypeStruct((16, 2), F32), in_s...  92.8 us

profile of v2, /device:TPU:1, one launch (start us, length us, event | category | flops | bytes accessed | tf_op | source)
XLA Modules:
  0.0 94.1 jit_solution(13150191210764882997)
XLA Ops:
  0.0 92.8 %grads_and_scores.1 = f32[16,2]{1,0:T(8,128)} custom-call(bf16[256,512]{1,0:T(8,128)(2,1)} %tok.1, bf16[256,512]{1,0:T(8,128)(2,1)} %cot.1, bf16[448,2048]{1,0:T(8,128)(2,1)} %bitcast.2, bf16[448,2048]{1,0:T(8,128)(2,1)} %bitcast.3, bf16[448,2048]{1,0:T(8,128)(2,1)} %wd.1, bf16[64,8192]{1,0:T(8,128)(2,1)} %mp.1, bf16[64,448]{1,0:T(8,128)(2,1)} %hp.1, ...), custom_call_target="tpu_custom_call" | custom-call | tf_op jit(solution)/shard_map/grads_and_scores/pallas_call | solution.py:367
  92.8 1.3 %copy.9 = f32[16,2]{0,1:T(2,128)} copy(f32[16,2]{1,0:T(8,128)} %grads_and_scores.1) | data formatting | bytes 256 | tf_op jit(solution)/shard_map/grads_and_scores/pallas_call | solution.py:367

commit v3 on v2

--- a/solution.py
+++ b/solution.py
@@ -11,6 +11,11 @@
 F32, BF16 = jnp.float32, jnp.bfloat16
 SEQ_LEN = 128
 NX, NY, NZ = 4, 4, 8
+SCHEDULE = (
+    "z0_0", "a1", "z0_1", "z0_2", "z0_3", "z1_0", "z0_4", "z1_1", "y0n", "m0", "x0", "y0s", "z1_2", "z1_3", "m1",
+    "x1", "z1_4", "y1n", "m2", "x2", "y1s", "m3",
+)
+PARTS = 1
 UP, DOWN = 2.0**40, 2.0**-20
 
 
@@ -78,13 +83,9 @@
     def wait(ref, sem):
         pltpu.make_async_copy(ref, ref, sem).wait()
 
-    @pl.when(k == 0)
-    def _():
-        local(tok, loc, ld_sem.at[0]).start()
-
-    @pl.when(k == 1)
-    def _():
-        local(cot, loc, ld_sem.at[0]).start()
+    own_loads = [local(tok, loc.at[0], ld_sem.at[0]), local(cot, loc.at[1], ld_sem.at[10])]
+    for c in own_loads:
+        c.start()
 
     depth = w_gu.shape[1]
     mp_own = mp.at[:, pl.ds(pl.multiple_of(x * depth, depth), depth)]
@@ -116,44 +117,54 @@
         pl.semaphore_signal(barrier, inc=1, device_id=p, device_id_type=MESH)
     pl.semaphore_wait(barrier, len(peers))
 
-    def rows(r, p, part=0, n=128):
-        return pl.ds(pl.multiple_of(r * 256 + p * 128 + part, 32), n)
-
-    def piece(r, p, v, part=0, n=64):
-        return full.at[k, rows(r, p, lax.rem(v, 2) * 64 + part, n), pl.ds(pl.multiple_of(v // 2 * 512, 512), 512)]
-
-    local(tok, loc, ld_sem.at[0]).wait()
+    def rows(i, p, part=0, n=128):
+        return pl.ds(pl.multiple_of(i * 256 + p * 128 + part, 32), n)
+
+    def piece(a, i, p, v, part=0, n=64):
+        at = rows(i, p, lax.rem(v, 2) * 64 + part, n)
+        return full.at[a, at, pl.ds(pl.multiple_of(v // 2 * 512, 512), 512)]
+
+    chunks = [(a, h, 64 // PARTS) for a in range(2) for h in range(0, 64, 64 // PARTS)]
+
+    def mine(n):
+        return 2 * n + 1 - k
+
+    for c in own_loads:
+        c.wait()
     xt = 2 * yhi + z // 4
     y2 = off(y, 2 * ylo + 3, NY)
     j = lax.rem(z, 4)
     me_p = lax.rem(y, 2)
+    away = lax.rem(x - xt + NX, NX)
     a_sends = []
     for n, (yt, u) in enumerate(((y2, 0), (y2, 1), (y, 0), (y, 1))):
         p = lax.rem(yt, 2)
-        src = loc.at[pl.ds(pl.multiple_of(p * 128 + u * 64, 64), 64)]
-        dst = piece(x, p, 2 * j + u)
+        slot = jnp.where(away == 2, 0, jnp.where(away == 0, 3, 2 - lax.rem(away // 2 + p, 2)))
         zt = lax.rem(z + j + u + NZ - 2, NZ)
-        c = remote(src, dst, a_snd.at[n], a_sem.at[x], dev(xt, yt, zt, k))
-        here = (xt == x) & (j + u == 2) if n >= 2 else None
-        a_sends.append((c, here))
-        if here is None:
-            c.start()
-        else:
-
-            @pl.when(jnp.logical_not(here))
+        here = (xt == x) & (j + u == 2) if n >= 2 else xt != xt
+        for m, (a, h, rows_) in enumerate(chunks):
+            src = loc.at[a, pl.ds(pl.multiple_of(p * 128 + u * 64 + h, 32), rows_)]
+            dst = piece(a, slot, p, 2 * j + u, h, rows_)
+            c = remote(src, dst, a_snd.at[n, m], a_sem.at[slot, m], dev(xt, yt, zt, k))
+            a_sends.append((m, c, here, slot, local(src, dst, a_sem.at[slot, m])))
+    a_sends.sort(key=lambda e: e[0])
+
+    def a_step(n):
+        for _, c, here, slot, stay in a_sends:
+
+            @pl.when((slot == mine(n)) & jnp.logical_not(here))
             def _(c=c):
                 c.start()
 
-            @pl.when(here)
-            def _(src=src, dst=dst):
-                local(src, dst, a_sem.at[x]).start()
-
+            @pl.when((slot == mine(n)) & here)
+            def _(stay=stay):
+                stay.start()
+
+    a_step(0)
     w_gu[896:960, :] = jnp.zeros((64, depth), BF16)
     hpz[0:64, :] = jnp.zeros((64, 448), BF16)
     hpz[128:192, :] = jnp.zeros((64, 448), BF16)
 
-    order = (2, 1, 3, 0)
-    rs = [off(x, o, NX) for o in order]
     zb = 4 * lax.rem(x, 2)
     w = lax.rem(z - zb + 2 + NZ, NZ)
     zp, zm = off(z, 1, NZ), off(z, NZ - 1, NZ)
@@ -162,60 +173,73 @@
     def place(o):
         return lax.rem(w + o + NZ, NZ)
 
-    def along_z(ref, up, r, s):
-        remote(ref, ref, snd_sem.at[0], z_sem.at[1 - up, r, s], dev(x, y, zp if up else zm, k)).start()
-
-    def along_y(r, v):
-        ref = piece(r, me_p, v)
+    def along_z(ref, to, i, way, s, m):
+        remote(ref, ref, snd_sem.at[0], z_sem.at[way, i, s, m], dev(x, y, to, k)).start()
+
+    def along_y(a, i, v, h, n):
+        ref = piece(a, i, me_p, v, h, n)
         to = jnp.where(lax.rem(v, 2) == 0, yp, ym)
-        remote(ref, ref, snd_sem.at[1], y_sem.at[r], dev(x, to, z, k)).start()
-
-    def z_step(i, s):
-        r = rs[i]
-        if s == 0:
-            own = piece(r, me_p, w)
-            wait(own, a_sem.at[r])
-            along_z(own, 1, r, 0)
-            along_z(own, 0, r, 0)
-            along_y(r, w)
-        elif s < 4:
-            for up in (1, 0):
-                v = place(-s if up else s)
-                got = piece(r, me_p, v)
-                wait(got, z_sem.at[1 - up, r, s - 1])
-                if s < 3:
-                    along_z(got, up, r, s)
-                else:
-                    along_z(piece(r, me_p, v, 0 if up else 32, 32), up, r, s)
-                along_y(r, v)
-        else:
-            v = place(4)
-            wait(piece(r, me_p, v, 0, 32), z_sem.at[0, r, 3])
-            wait(piece(r, me_p, v, 32, 32), z_sem.at[1, r, 3])
-            along_y(r, v)
-            ref = full.at[k, rows(r, me_p)]
-            remote(ref, ref, snd_sem.at[2], d_sem.at[r], dev(x, y, z, sib)).start()
-
-    def y_step(i):
-        r = rs[i]
-        ref = full.at[k, rows(r, 1 - me_p)]
-        wait(ref, y_sem.at[r])
-        remote(ref, ref, snd_sem.at[2], d_sem.at[r], dev(x, y, z, sib)).start()
+        remote(ref, ref, snd_sem.at[1], y_sem.at[i, a], dev(x, to, z, k)).start()
+
+    def to_sibling(a, i, p):
+        ref = full.at[a, rows(i, p)]
+        remote(ref, ref, snd_sem.at[2], d_sem.at[i, a], dev(x, y, z, sib)).start()
+
+    def z_step(n, s):
+        i = mine(n)
+        for m, (a, h, rows_) in enumerate(chunks):
+            if s == 0:
+                own = piece(a, i, me_p, w, h, rows_)
+                wait(own, a_sem.at[i, m])
+                along_z(own, zp, i, 0, 0, m)
+                along_z(own, zm, i, 1, 0, m)
+                along_y(a, i, w, h, rows_)
+            elif s < 4:
+                for way in range(2):
+                    v = place(s if way else -s)
+                    got = piece(a, i, me_p, v, h, rows_)
+                    wait(got, z_sem.at[way, i, s - 1, m])
+                    to = zm if way else zp
+                    if s < 3:
+                        along_z(got, to, i, way, s, m)
+                    elif PARTS == 1:
+                        along_z(piece(a, i, me_p, v, 32 * way, 32), to, i, way, s, m)
+                    elif h == 32 * way:
+                        along_z(got, to, i, way, s, m)
+                    along_y(a, i, v, h, rows_)
+            else:
+                v = place(4)
+                for way in range(2):
+                    if PARTS == 1 or h == 32 * way:
+                        wait(piece(a, i, me_p, v, 32 * way, 32), z_sem.at[way, i, 3, m])
+                along_y(a, i, v, h, rows_)
+                if m % PARTS == PARTS - 1:
+                    to_sibling(a, i, me_p)
+
+    def y_step(n, who):
+        @pl.when(k == who)
+        def _():
+            i = mine(n)
+            for a in range(2):
+                wait(full.at[a, rows(i, 1 - me_p)], y_sem.at[i, a])
+                to_sibling(a, i, 1 - me_p)
 
     slots = (0, 1, 2, 0)
 
-    def block(i):
-        return pl.ds(pl.multiple_of(rs[i] * 256, 256), 256)
-
-    def multiply_gu(i):
-        wait(full.at[sib, block(i)], d_sem.at[rs[i]])
-        acc[slots[i], :, 0:1024] = dot_t(full[0, block(i), :], w_gu[...])
-
     left_lanes = lax.broadcasted_iota(jnp.int32, (256, 128), 1) < 64
 
-    def multiply_b(i):
-        slot = slots[i]
-        acc[slot, :, 1024:1536] = dot_t(full[1, block(i), :], w_b[...])
+    def multiply(i):
+        block, slot = pl.ds(i * 256, 256), slots[i]
+
+        def arrive(a):
+            @pl.when(k == i % 2)
+            def _():
+                wait(full.at[a, block], d_sem.at[i, a])
+
+        arrive(0)
+        acc[slot, :, 0:1024] = dot_t(full[0, block, :], w_gu[...])
+        arrive(1)
+        acc[slot, :, 1024:1536] = dot_t(full[1, block, :], w_b[...])
         both = acc[slot, :, 1408:1536]
         acc[slot, :, 896:1024] = jnp.where(left_lanes | (k == 1), both, acc[slot, :, 896:1024])
 
@@ -242,42 +266,35 @@
             x_put(0, 0, rh.at[0], rh_sem.at[0], xp)
             x_put(0, 1, rh.at[1], rh_sem.at[1], xm)
         elif i == 1:
+            x_put(1, 0, rx.at[1, top], rx_sem.at[1, 0], xm)
             x_put(1, 1, rx.at[0, low], rx_sem.at[0, 1], xp)
-        elif i == 2:
-            x_put(2, 0, rx.at[1, top], rx_sem.at[1, 0], xm)
-
-    def x_last(h):
-        wait(rh.at[h], rh_sem.at[h])
-        if h == 0:
-            x_put(1, 0, rx.at[0, top], rx_sem.at[0, 0], xp, rh[0])
         else:
+            wait(rh.at[0], rh_sem.at[0])
+            x_put(2, 0, rx.at[0, top], rx_sem.at[0, 0], xp, rh[0])
+            wait(rh.at[1], rh_sem.at[1])
             x_put(2, 1, rx.at[1, low], rx_sem.at[1, 1], xm, rh[1])
 
-    events = []
-    starts = (0, 1, 3, 5)
-    for i, at in enumerate(starts):
-        for s in range(5):
-            events.append((at + s, 0, i, "z%d_%d" % (i, s), functools.partial(z_step, i, s)))
-        events.append((at + 5, 1, i, "y%d" % i, functools.partial(y_step, i)))
-        events.append((at + 6, 2, i, "gu%d" % i, functools.partial(multiply_gu, i)))
-        events.append((at + 7, 2, i, "b%d" % i, functools.partial(multiply_b, i)))
-        events.append((at + 7, 3, i, "x%d" % i, functools.partial(x_step, i)))
-    events.append((11, 4, 0, "xl0", functools.partial(x_last, 0)))
-    events.append((12, 4, 1, "xl1", functools.partial(x_last, 1)))
-    events.sort(key=lambda e: e[:3])
-    waited = False
-    for e in events:
-        if e[3] == "gu0":
+    steps = {"a1": functools.partial(a_step, 1)}
+    for n in range(2):
+        for q in range(5):
+            steps["z%d_%d" % (n, q)] = functools.partial(z_step, n, q)
+        steps["y%dn" % n] = functools.partial(y_step, n, 1)
+        steps["y%ds" % n] = functools.partial(y_step, n, 0)
+    for i in range(4):
+        steps["m%d" % i] = functools.partial(multiply, i)
+    for i in range(3):
+        steps["x%d" % i] = functools.partial(x_step, i)
+    for name in SCHEDULE:
+        if name == "m0":
             for c in loads:
                 c.wait()
-        with jax.named_scope(e[3]):
-            e[4]()
-
-    for s in range(2):
+        with jax.named_scope(name):
+            steps[name]()
+
+    for n, s in ((1, 0), (0, 1), (0, 0), (1, 1)):
         part = pl.ds(s * 128, 128)
-        wait(rx.at[0, part], rx_sem.at[0, s])
-        wait(rx.at[1, part], rx_sem.at[1, s])
-        acc[0, part, 0:1408] = acc[0, part, 0:1408] + decoded(rx[0, part]) + decoded(rx[1, part])
+        wait(rx.at[n, part], rx_sem.at[n, s])
+        acc[0, part, 0:1408] = acc[0, part, 0:1408] + decoded(rx[n, part])
     ml[0] = acc[0, :, 896:1024]
     model = remote(ml.at[0], ml.at[1], ml_sem.at[0], ml_sem.at[1], dev(x, y, z, sib))
     model.start()
@@ -338,17 +355,14 @@
         q = qv[:, p * 128 : (p + 1) * 128].astype(F32)
         for s in range(2):
             sums[s] += q * gs[s, p : p + 1, :]
-    two = lax.broadcasted_iota(jnp.int32, (16, 2), 1)
-    out[...] = jnp.where(two == 0, sums[0].sum(1, keepdims=True), sums[1].sum(1, keepdims=True))
-
-    for c, here in a_sends:
-        if here is None:
+    for s in range(2):
+        out[s, :] = sums[s].sum(1)
+
+    for _, c, here, slot, _ in a_sends:
+
+        @pl.when((lax.rem(slot, 2) == 1 - k) & jnp.logical_not(here))
+        def _(c=c):
             c.wait_send()
-        else:
-
-            @pl.when(jnp.logical_not(here))
-            def _(c=c):
-                c.wait_send()
 
     wait(full.at[0, pl.ds(0, 448)], snd_sem.at[0])
     wait(full.at[0, pl.ds(0, 512)], snd_sem.at[1])
@@ -366,11 +380,11 @@
     dma = pltpu.SemaphoreType.DMA
     return pl.pallas_call(
         kernel,
-        out_shape=jax.ShapeDtypeStruct((16, 2), F32),
+        out_shape=jax.ShapeDtypeStruct((2, 16), F32),
         in_specs=[any_] * 8,
         out_specs=pl.BlockSpec(memory_space=pltpu.VMEM),
         scratch_shapes=[
-            pltpu.VMEM((256, 512), BF16),
+            pltpu.VMEM((2, 256, 512), BF16),
             pltpu.VMEM((2, 1024, depth), BF16),
             pltpu.VMEM((1024, depth), BF16),
             pltpu.VMEM((512, depth), BF16),
@@ -387,13 +401,13 @@
             pltpu.VMEM((24, 128), F32),
             pltpu.VMEM((7, 24, 128), F32),
             pltpu.VMEM((2, 96, 128), F32),
+            dma((11,)),
+            dma((4, 4)),
+            dma((2, 4, 4, 4)),
+            dma((4, 2)),
+            dma((4, 2)),
             dma((10,)),
-            dma((4,)),
-            dma((2, 4, 4)),
-            dma((4,)),
-            dma((4,)),
-            dma((10,)),
-            dma((4,)),
+            dma((4, 4)),
             dma((6,)),
             dma((2,)),
             dma((2, 2)),
@@ -406,7 +420,7 @@
             collective_id=0, has_side_effects=True, vmem_limit_bytes=60 * 2**20
         ),
         name="grads_and_scores",
-    )(tok, cot, wg, wu, wd, mp, hp, qs)
+    )(tok, cot, wg, wu, wd, mp, hp, qs).T
 
 
 def solution(mesh):

time: 94.2 us -> 87 us (0.924)
  Pallas kernels: 92.8 us -> 85.7 us
    pallas_call x1, Pallas kernels: 92.8 us -> 85.7 us  [on_device(): pl.pallas_call(kernel, out_shape=jax.ShapeDtypeStruct((2, 16), F32), in_s...]
    pallas_call x1 -> x0, local copies, waits for them, and re-layouts: 1.33 us -> none  [on_device(): pl.pallas_call(kernel, out_shape=jax.ShapeDtypeStruct((16, 2), F32), in_s...]
    unnamed x0 -> x1, local copies, waits for them, and re-layouts: none -> 1.24 us
where the time goes in v3:
time: 87 us; the launch traced here: 86.9 us
  Pallas kernels  85.7 us (99%)
  local copies, waits for them, and re-layouts  1.24 us (1%)
    pallas_call x1, Pallas kernels, on_device(): pl.pallas_call(kernel, out_shape=jax.ShapeDtypeStruct((2, 16), F32), in_s...  85.7 us

profile of v3, /device:TPU:1, one launch (start us, length us, event | category | flops | bytes accessed | tf_op | source)
XLA Modules:
  0.0 86.9 jit_solution(16230030587392323931)
XLA Ops:
  0.0 85.7 %grads_and_scores.1 = f32[2,16]{1,0:T(2,128)} custom-call(bf16[256,512]{1,0:T(8,128)(2,1)} %tok.1, bf16[256,512]{1,0:T(8,128)(2,1)} %cot.1, bf16[448,2048]{1,0:T(8,128)(2,1)} %bitcast.3, bf16[448,2048]{1,0:T(8,128)(2,1)} %bitcast.4, bf16[448,2048]{1,0:T(8,128)(2,1)} %wd.1, bf16[64,8192]{1,0:T(8,128)(2,1)} %mp.1, bf16[64,448]{1,0:T(8,128)(2,1)} %hp.1, ...), custom_call_target="tpu_custom_call" | custom-call | tf_op jit(solution)/shard_map/grads_and_scores/pallas_call | solution.py:381
  85.7 1.2 %copy.10 = f32[16,2]{0,1:T(2,128)} copy(f32[16,2]{0,1:T(2,128)} %bitcast.5) | data formatting | bytes 256
